TPU v7x, 32 devices: a whole 2x2x4 slice. The times are simulated.
32 devices in a mesh: grp: 8 (over y, x, core), col: 4 (over z).
Axes of the slice: x: 2, y: 2, z: 4, core: 2. Of those that a mesh axis runs over, the one named last changes fastest.
Arguments:
- old_tables: bfloat16 [32, 128, 32768], P(('grp', 'col')), may hold values from -3 to 3
- table_rows: int32 [32], replicated, may hold values from 4096 to 32768, as said below
- old_plan: int32 [32], replicated, may hold values from 0 to 31, each once
- new_plan: int32 [32], replicated, may hold values from 0 to 31, each once
- ids: int32 [256, 32, 16], P(('grp', 'col')), may hold values from 0 to 32767, as said below
- bag_len: int32 [256, 32], P(('grp', 'col')), may hold values from 1 to 16
Outputs:
- new_tables: bfloat16 [32, 128, 32768], P('grp', 'col')
- pooled: float32 [256, 32, 128], P(('grp', 'col'))
Inputs may be any that keep to these rules, and one draw needn't show every extreme that they name: table_rows[t] is a multiple of 4096, and some table has exactly 32768 rows. `ids`: every id of table t lies below table_rows[t].
All inputs are finite; a program needn't handle non-finite values.
Results may differ from a plain program's by a relative error of at most 0.001.
Values may be sent and summed in bfloat16 or wider, within the bound.
A program may use at most 128 MiB of HBM per device.

v0:
```python
import jax
import jax.numpy as jnp
from jax import lax
from jax.sharding import PartitionSpec as P


def invert(permutation):
    entries = permutation.shape[0]
    across = lax.broadcasted_iota(jnp.int32, (entries, entries), 1)
    down = lax.broadcasted_iota(jnp.int32, (entries, entries), 0)
    return jnp.sum(jnp.where(permutation[None, :] == down, across, 0), axis=1)


def pool_rows(table_cols, marked):
    columns = table_cols.shape[0]
    safe_ids = jnp.maximum(marked, 0).reshape(-1)
    weights = (marked >= 0).astype(jnp.float32)
    picked = (
        jnp.take(table_cols, safe_ids, axis=1)
        .reshape(columns, marked.shape[0], marked.shape[1])
        .astype(jnp.float32)
    )
    return jnp.sum(picked * weights[None, :, :], axis=2)


def reorder_blocks(spread, source_rows):
    count = spread.shape[0]
    across = lax.broadcasted_iota(jnp.int32, (count, count), 1)
    selector = (source_rows[:, None] == across).astype(spread.dtype)
    flat = spread.reshape(count, -1)
    picked = jnp.dot(selector, flat, preferred_element_type=jnp.float32).astype(spread.dtype)
    return picked.reshape(spread.shape)


def body(old_tables, table_rows, old_plan, new_plan, ids, bag_len):
    group_count = lax.axis_size("grp")
    col_count = lax.axis_size("col")
    device_count = group_count * col_count
    full_width = old_tables.shape[1]
    table_len = old_tables.shape[2]
    row_block = table_len // device_count
    narrow = full_width // col_count
    per_group = new_plan.shape[0] // group_count
    bag_size = ids.shape[2]
    own_slot = lax.axis_index("grp") * col_count + lax.axis_index("col")
    own_table = old_plan[own_slot]
    row_limit = table_rows[own_table]
    row_iota = lax.broadcasted_iota(jnp.int32, (1, table_len), 1)
    owned_table = old_tables[0] * (row_iota < row_limit).astype(old_tables.dtype)
    spread = lax.all_to_all(
        owned_table.reshape(full_width, device_count, row_block),
        ("grp", "col"),
        split_axis=1,
        concat_axis=0,
        tiled=True,
    )
    spread = spread.reshape(device_count * col_count, narrow, row_block)
    old_inverse = invert(old_plan)
    source_slot = old_inverse[new_plan].reshape(group_count, 1, per_group)
    source_rows = (
        source_slot * col_count + lax.broadcasted_iota(jnp.int32, (1, col_count, 1), 1)
    ).reshape(-1)
    blocks = reorder_blocks(spread, source_rows)
    direct = lax.all_to_all(
        blocks.reshape(device_count, per_group, narrow, row_block),
        ("grp", "col"),
        split_axis=0,
        concat_axis=3,
        tiled=True,
    )
    new_local = direct.reshape(per_group, narrow, table_len)
    bag_iota = lax.broadcasted_iota(jnp.int32, (1, 1, bag_size), 2)
    marked = jnp.where(bag_iota < bag_len[:, :, None], ids, -1)
    by_slot = jnp.take(marked, old_plan, axis=1)
    own_ids = lax.all_to_all(
        by_slot, ("grp", "col"), split_axis=1, concat_axis=0, tiled=True
    ).reshape(-1, bag_size)
    partial_value = pool_rows(owned_table, own_ids)
    returned = lax.all_to_all(
        partial_value.reshape(1, full_width, -1),
        ("grp", "col"),
        split_axis=2,
        concat_axis=0,
        tiled=True,
    )
    by_table = jnp.take(returned, old_inverse, axis=0)
    pooled = jnp.transpose(by_table, (2, 0, 1))
    return (new_local, pooled)


def solution(mesh):
    return jax.shard_map(
        body,
        mesh=mesh,
        in_specs=(
            P(("grp", "col"), None, None),
            P(),
            P(),
            P(),
            P(("grp", "col"), None, None),
            P(("grp", "col"), None),
        ),
        out_specs=(P("grp", "col", None), P(("grp", "col"), None, None)),
        check_vma=False,
    )
```

profile of v0, /device:TPU:9, one launch (start us, length us, event | category | flops | bytes accessed | tf_op | source)
XLA Modules:
  0.0 492.5 jit_solution(5518799861332294195)
XLA Ops:
  0.6 0.7 compare_select_fusion.1
  1.3 0.7 compare_and_fusion
  2.0 0.9 copy.25
  2.9 0.8 copy.24
  3.8 0.6 gather_fusion.1
  4.5 0.7 reshape.168
  5.2 6.3 %all-to-all-start.2 = ((s32[32,1,128]{2,1,0:T(1,128)}), s32[32,1,128]{2,1,0:T(1,128)S(1)}, u32[]{:S(2)}, u32[]{:S(2)}) async-start(s32[32,1,128]{2,1,0:T(1,128)} %reshape.168), calls=%async_computation.2 | async-start | bytes 32768 | tf_op jit(solution)/shard_map/all_to_all | solution.py:75
  11.5 1.2 dynamic_slice.6
  14.7 1.3 dynamic_slice.7
  16.0 0.7 fusion
  16.7 12.4 %copy.28 = bf16[16,8,32,1024]{3,2,1,0:T(8,128)(2,1)} copy(bf16[16,8,32,1024]{3,1,2,0:T(8,128)(2,1)} %bitcast.70) | data formatting | bytes 16777216
  29.1 16.0 %copy_multiply_fusion = bf16[128,32,1024]{2,0,1:T(8,128)(2,1)} fusion(bf16[128,32,1024]{2,1,0:T(8,128)(2,1)} %bitcast.72, bf16[32,1024]{1,0:T(8,128)(2,1)S(1)} %fusion), kind=kLoop, calls=%fused_computation.6 | loop fusion | flops 4194304 | bytes 16842752 | tf_op jit(solution)/shard_map/mul | solution.py:49
  45.1 5.9 %all-to-all-start = ((bf16[128,32,1024]{2,0,1:T(8,128)(2,1)}), bf16[128,32,1024]{2,0,1:T(8,128)(2,1)}, u32[]{:S(2)}, u32[]{:S(2)}) async-start(bf16[128,32,1024]{2,0,1:T(8,128)(2,1)} %copy_multiply_fusion), calls=%async_computation | async-start | bytes 16777216 | tf_op jit(solution)/shard_map/all_to_all | solution.py:50
  51.0 11.9 %copy.26 = bf16[1,128,32768]{1,2,0:T(8,128)(2,1)} copy(bf16[1,128,32768]{2,1,0:T(8,128)(2,1)} %param.6) | data formatting | bytes 16777216 | tf_op args[0]
  63.0 0.7 gather_fusion
  64.0 0.7 fusion.2
  64.6 8.6 %bitcast_multiply_fusion = bf16[128,32768]{0,1:T(8,128)(2,1)} fusion(bf16[1,128,32768]{1,2,0:T(8,128)(2,1)} %copy.26, bf16[32768]{0:T(1024)(128)(2,1)S(1)} %fusion.2), kind=kLoop, calls=%fused_computation.5 | loop fusion | flops 4194304 | bytes 16842752 | tf_op jit(solution)/shard_map/mul | solution.py:49
  73.2 0.5 broadcast.144
  73.7 0.7 reduce
  74.6 15.5 %gather_fusion.2 = bf16[4096,128]{1,0:T(8,128)(2,1)S(1)} fusion(bf16[128,32768]{0,1:T(8,128)(2,1)} %bitcast_multiply_fusion, s32[4096]{0:T(1024)S(1)} %broadcast_clamp_fusion), kind=kCustom, calls=%fused_computation.2 | custom fusion | bytes 2113536 | tf_op jit(solution)/shard_map/jit(_take)/gather | solution.py:19
  90.1 2.2 multiply_reduce_fusion
  92.3 144.8 %all-to-all-done = bf16[128,32,1024]{2,0,1:T(8,128)(2,1)} async-done(((bf16[128,32,1024]{2,0,1:T(8,128)(2,1)}), bf16[128,32,1024]{2,0,1:T(8,128)(2,1)}, u32[]{:S(2)}, u32[]{:S(2)}) %all-to-all-start) | async-done | bytes 8388640 | tf_op jit(solution)/shard_map/all_to_all | solution.py:50
  237.1 3.7 all-to-all-start.3
  240.8 13.4 %reshape_reshape.6 = bf16[128,32768]{1,0:T(8,128)(2,1)} reshape(bf16[32,128,1,1024]{3,1,0,2:T(8,128)(2,1)} %bitcast.3) | data formatting | bytes 16777216 | tf_op jit(solution)/shard_map/reshape;reshape | solution.py:30
  254.2 9.0 %convolution_convert_fusion = bf16[128,32768]{1,0:T(8,128)(2,1)} fusion(bf16[128,32768]{1,0:T(8,128)(2,1)} %reshape_reshape.6, s32[128]{0:T(128)S(1)} %add.73), kind=kOutput, calls=%fused_computation.4 | convolution fusion | flops 1077952512 | bytes 16777728 | tf_op jit(solution)/shard_map/dot_general | solution.py:31
  263.2 12.4 %copy.29 = bf16[16,8,32,1024]{3,2,1,0:T(8,128)(2,1)} copy(bf16[16,8,32,1024]{3,1,2,0:T(8,128)(2,1)} %bitcast.69) | data formatting | bytes 16777216
  275.6 5.9 %all-to-all-start.1 = ((bf16[32,4,32,1024]{3,2,1,0:T(8,128)(2,1)}), bf16[32,4,32,1024]{3,2,1,0:T(8,128)(2,1)}, u32[]{:S(2)}, u32[]{:S(2)}) async-start(bf16[32,4,32,1024]{3,2,1,0:T(8,128)(2,1)} %bitcast.71), calls=%async_computation.1 | async-start | bytes 16777216 | tf_op jit(solution)/shard_map/all_to_all | solution.py:64
  281.6 0.6 gather_fusion.3
  282.3 0.7 copy.27
  282.9 184.7 %all-to-all-done.1 = bf16[32,4,32,1024]{3,2,1,0:T(8,128)(2,1)} async-done(((bf16[32,4,32,1024]{3,2,1,0:T(8,128)(2,1)}), bf16[32,4,32,1024]{3,2,1,0:T(8,128)(2,1)}, u32[]{:S(2)}, u32[]{:S(2)}) %all-to-all-start.1) | async-done | bytes 8388640 | tf_op jit(solution)/shard_map/all_to_all | solution.py:64
  467.7 11.4 %copy.23 = bf16[1,4,32,32,1024]{4,3,2,1,0:T(8,128)(2,1)} copy(bf16[1,4,32,32,1024]{4,2,1,3,0:T(8,128)(2,1)} %bitcast.5) | data formatting | bytes 16777216 | tf_op jit(solution)/shard_map/all_to_all | solution.py:64
  479.1 13.4 %reshape.129 = bf16[4,32,32768]{2,1,0:T(8,128)(2,1)} reshape(bf16[1,4,32,32,1024]{4,3,2,1,0:T(8,128)(2,1)} %copy.23) | data formatting | bytes 16777216 | tf_op jit(solution)/shard_map/reshape | solution.py:71
  (25 shorter events, 0.9 us)
Async XLA Ops:
  5.2 39.9 %all-to-all-start.2 = ((s32[32,1,128]{2,1,0:T(1,128)}), s32[32,1,128]{2,1,0:T(1,128)S(1)}, u32[]{:S(2)}, u32[]{:S(2)}) async-start(s32[32,1,128]{2,1,0:T(1,128)} %reshape.168), calls=%async_computation.2 | async-start | bytes 32768 | tf_op jit(solution)/shard_map/all_to_all | solution.py:75
  45.1 192.0 %all-to-all-start = ((bf16[128,32,1024]{2,0,1:T(8,128)(2,1)}), bf16[128,32,1024]{2,0,1:T(8,128)(2,1)}, u32[]{:S(2)}, u32[]{:S(2)}) async-start(bf16[128,32,1024]{2,0,1:T(8,128)(2,1)} %copy_multiply_fusion), calls=%async_computation | async-start | bytes 16777216 | tf_op jit(solution)/shard_map/all_to_all | solution.py:50
  51.0 11.9 %copy-start = (s32[32]{0:T(128)S(1)}, s32[32]{0:T(128)}, u32[]{:S(2)}) copy-start(s32[32]{0:T(128)} %param.9) | copy-start | bytes 388
  51.0 11.9 %copy-start.1 = (s32[32]{0:T(128)S(1)}, s32[32]{0:T(128)}, u32[]{:S(2)}) copy-start(s32[32]{0:T(128)} %param.8) | copy-start | bytes 388
  237.1 38.5 %all-to-all-start.3 = ((f32[1,128,256]{1,0,2:T(1,128)}), f32[1,128,256]{1,0,2:T(1,128)S(1)}, u32[]{:S(2)}, u32[]{:S(2)}) async-start(f32[1,128,256]{1,0,2:T(1,128)} %bitcast.18), calls=%async_computation.3 | async-start | bytes 262144 | tf_op jit(solution)/shard_map/all_to_all | solution.py:79
  275.6 192.0 %all-to-all-start.1 = ((bf16[32,4,32,1024]{3,2,1,0:T(8,128)(2,1)}), bf16[32,4,32,1024]{3,2,1,0:T(8,128)(2,1)}, u32[]{:S(2)}, u32[]{:S(2)}) async-start(bf16[32,4,32,1024]{3,2,1,0:T(8,128)(2,1)} %bitcast.71), calls=%async_computation.1 | async-start | bytes 16777216 | tf_op jit(solution)/shard_map/all_to_all | solution.py:64
where the time goes:
time: 494 us; the launch traced here: 492 us
  waiting for transfers between devices  329 us (67%)
  local copies, waits for them, and re-layouts  98.9 us (20%)
  other arithmetic  30.6 us (6%)
  starting transfers between devices  21.8 us (4%)
  matrix products  8.98 us (2%)
    all_to_all x1, waiting for transfers between devices, body(): lax.all_to_all(blocks.reshape(device_count, per_group, narrow, row_block)...  185 us
    all_to_all x1, waiting for transfers between devices, body(): lax.all_to_all(owned_table.reshape(full_width, device_count, row_block),...  145 us
    unnamed x12, local copies, waits for them, and re-layouts  39.9 us
    mul x2, other arithmetic, body(): old_tables[0] * (row_iota < row_limit).astype(old_tables.dtype)  24.6 us
    gather x1, local copies, waits for them, and re-layouts, pool_rows(): jnp.take(table_cols, safe_ids, axis=1)  15.5 us
    another operation x1, local copies, waits for them, and re-layouts, reorder_blocks(): flat = spread.reshape(count, -1)  13.4 us
    reshape x1, local copies, waits for them, and re-layouts, body(): new_local = direct.reshape(per_group, narrow, table_len)  13.4 us
    all_to_all x1, local copies, waits for them, and re-layouts, body(): lax.all_to_all(blocks.reshape(device_count, per_group, narrow, row_block)...  11.4 us
  transfers between devices with their start and end apart: 4, of which 2 were waited for; matrix products, arithmetic and copies ran while one was open for 22% of the time, Pallas kernels for 0%

commit v1 on v0

--- a/solution.py
+++ b/solution.py
@@ -47,12 +47,20 @@
     row_limit = table_rows[own_table]
     row_iota = lax.broadcasted_iota(jnp.int32, (1, table_len), 1)
     owned_table = old_tables[0] * (row_iota < row_limit).astype(old_tables.dtype)
-    spread = lax.all_to_all(
-        owned_table.reshape(full_width, device_count, row_block),
-        ("grp", "col"),
-        split_axis=1,
-        concat_axis=0,
-        tiled=True,
+    spread = jnp.concatenate(
+        lax.all_to_all(
+            jnp.stack(
+                jnp.split(
+                    owned_table.reshape(full_width, device_count, row_block),
+                    lax.axis_size(("grp", "col")),
+                    axis=1,
+                )
+            ),
+            ("grp", "col"),
+            0,
+            0,
+        ),
+        axis=0,
     )
     spread = spread.reshape(device_count * col_count, narrow, row_block)
     old_inverse = invert(old_plan)

time: 494 us -> 520 us (1.053)
  local copies, waits for them, and re-layouts: 98.9 us -> 121 us
  waiting for transfers between devices: 329 us -> 341 us
  other arithmetic: 30.6 us -> 21.6 us
    all_to_all x1, waiting for transfers between devices: 145 us -> 157 us  [body(): lax.all_to_all(jnp.stack(jnp.split(owned_table.reshape(full_width, device...]
    all_to_all x0 -> x1, local copies, waits for them, and re-layouts: none -> 11.9 us  [body(): lax.all_to_all(jnp.stack(jnp.split(owned_table.reshape(full_width, device...]
    unnamed x12 -> x40, local copies, waits for them, and re-layouts: 39.9 us -> 49.8 us
    mul x2, other arithmetic: 24.6 us -> 14.9 us  [body(): old_tables[0] * (row_iota < row_limit).astype(old_tables.dtype)]
  transfers between devices with their start and end apart: 4 -> 4, of which waited for: 2 -> 2; matrix products, arithmetic and copies ran while one was open for 22% -> 24% of each run, Pallas kernels for 0% -> 0%
where the time goes in v1:
time: 520 us; the launch traced here: 518 us
  waiting for transfers between devices  341 us (66%)
  local copies, waits for them, and re-layouts  121 us (23%)
  starting transfers between devices  21.8 us (4%)
  other arithmetic  21.6 us (4%)
  matrix products  9.15 us (2%)
    all_to_all x1, waiting for transfers between devices, body(): lax.all_to_all(blocks.reshape(device_count, per_group, narrow, row_block)...  185 us
    all_to_all x1, waiting for transfers between devices, body(): lax.all_to_all(jnp.stack(jnp.split(owned_table.reshape(full_width, device...  157 us
    unnamed x40, local copies, waits for them, and re-layouts  49.8 us
    gather x1, local copies, waits for them, and re-layouts, pool_rows(): jnp.take(table_cols, safe_ids, axis=1)  15.5 us
    mul x2, other arithmetic, body(): old_tables[0] * (row_iota < row_limit).astype(old_tables.dtype)  14.9 us
    another operation x1, local copies, waits for them, and re-layouts, reorder_blocks(): flat = spread.reshape(count, -1)  13.5 us
    reshape x1, local copies, waits for them, and re-layouts, body(): new_local = direct.reshape(per_group, narrow, table_len)  13.4 us
    all_to_all x1, local copies, waits for them, and re-layouts, body(): lax.all_to_all(jnp.stack(jnp.split(owned_table.reshape(full_width, device...  11.9 us
  transfers between devices with their start and end apart: 4, of which 2 were waited for; matrix products, arithmetic and copies ran while one was open for 24% of the time, Pallas kernels for 0%

profile of v1, /device:TPU:9, one launch (start us, length us, event | category | flops | bytes accessed | tf_op | source)
XLA Modules:
  0.0 518.2 jit_solution(194304524486270480)
XLA Ops:
  2.6 0.8 copy.77
  3.4 0.9 copy.78
  5.9 6.3 %all-to-all-start.2 = ((s32[32,1,128]{2,1,0:T(1,128)}), s32[32,1,128]{2,1,0:T(1,128)S(1)}, u32[]{:S(2)}, u32[]{:S(2)}) async-start(s32[32,1,128]{2,1,0:T(1,128)} %reshape.167), calls=%async_computation.2 | async-start | bytes 32768 | tf_op jit(solution)/shard_map/all_to_all | solution.py:83
  12.2 1.2 dynamic_slice.6
  15.4 1.3 dynamic_slice.7
  17.3 11.9 %copy.72 = bf16[1,128,32768]{1,2,0:T(8,128)(2,1)} copy(bf16[1,128,32768]{2,1,0:T(8,128)(2,1)} %param.6) | data formatting | bytes 16777216 | tf_op args[0]
  29.2 6.4 %broadcast_multiply_fusion = bf16[128,32,1024]{0,2,1:T(8,128)(2,1)S(1)} fusion(bf16[128,32,1024]{0,2,1:T(8,128)(2,1)} %bitcast.191, bf16[32,1024]{1,0:T(8,128)(2,1)S(1)} %fusion.32), kind=kLoop, calls=%fused_computation.6 | loop fusion | flops 4194304 | bytes 16842752 | tf_op jit(solution)/shard_map/mul | solution.py:49
  35.6 0.7 fusion.31
  36.3 0.7 fusion.30
  37.1 0.7 fusion.29
  37.8 0.7 fusion.28
  40.0 0.7 fusion.25
  41.4 0.7 fusion.23
  42.9 0.7 fusion.21
  48.7 0.7 fusion.13
  53.7 0.7 fusion.6
  55.2 0.7 fusion.4
  58.1 0.7 fusion
  58.8 5.9 %all-to-all-start = ((bf16[32,128,1,1024]{1,3,2,0:T(8,128)(2,1)}), bf16[32,128,1,1024]{1,3,2,0:T(8,128)(2,1)}, u32[]{:S(2)}, u32[]{:S(2)}) async-start(bf16[32,128,1,1024]{1,3,2,0:T(8,128)(2,1)} %fusion), calls=%async_computation | async-start | bytes 16777216 | tf_op jit(solution)/shard_map/all_to_all | solution.py:51
  66.4 8.6 %bitcast_multiply_fusion = bf16[128,32768]{0,1:T(8,128)(2,1)} fusion(bf16[1,128,32768]{1,2,0:T(8,128)(2,1)} %copy.72, bf16[32768]{0:T(1024)(128)(2,1)S(1)} %fusion.34), kind=kLoop, calls=%fused_computation.5 | loop fusion | flops 4194304 | bytes 16842752 | tf_op jit(solution)/shard_map/mul | solution.py:49
  76.4 15.5 %gather_fusion.2 = bf16[4096,128]{1,0:T(8,128)(2,1)S(1)} fusion(bf16[128,32768]{0,1:T(8,128)(2,1)} %bitcast_multiply_fusion, s32[4096]{0:T(1024)S(1)} %broadcast_clamp_fusion), kind=kCustom, calls=%fused_computation.2 | custom fusion | bytes 2113536 | tf_op jit(solution)/shard_map/jit(_take)/gather | solution.py:19
  92.0 2.2 multiply_reduce_fusion
  94.1 156.7 %all-to-all-done = bf16[32,128,1,1024]{1,3,2,0:T(8,128)(2,1)} async-done(((bf16[32,128,1,1024]{1,3,2,0:T(8,128)(2,1)}), bf16[32,128,1,1024]{1,3,2,0:T(8,128)(2,1)}, u32[]{:S(2)}, u32[]{:S(2)}) %all-to-all-start) | async-done | bytes 8388640 | tf_op jit(solution)/shard_map/all_to_all | solution.py:51
  250.9 3.7 all-to-all-start.3
  254.6 11.9 %copy.75 = bf16[32,128,1,1024]{3,1,0,2:T(8,128)(2,1)} copy(bf16[32,128,1,1024]{1,3,2,0:T(8,128)(2,1)} %all-to-all-done) | data formatting | bytes 16777216 | tf_op jit(solution)/shard_map/all_to_all | solution.py:51
  266.5 13.5 %reshape_reshape_reshape.3 = bf16[128,32768]{1,0:T(8,128)(2,1)} reshape(bf16[32,128,1,1024]{3,1,0,2:T(8,128)(2,1)} %copy.75) | data formatting | bytes 16777216 | tf_op jit(solution)/shard_map/reshape;reshape;reshape | solution.py:30
  280.0 9.2 %convolution_convert_fusion = bf16[128,32768]{1,0:T(8,128)(2,1)} fusion(bf16[128,32768]{1,0:T(8,128)(2,1)} %reshape_reshape_reshape.3, s32[128]{0:T(128)S(1)} %add.73), kind=kOutput, calls=%fused_computation.4 | convolution fusion | flops 1077952512 | bytes 16777728 | tf_op jit(solution)/shard_map/dot_general | solution.py:31
  289.1 12.2 %copy.82 = bf16[16,8,32,1024]{3,2,1,0:T(8,128)(2,1)} copy(bf16[16,8,32,1024]{3,1,2,0:T(8,128)(2,1)} %bitcast.193) | data formatting | bytes 16777216
  301.4 5.9 %all-to-all-start.1 = ((bf16[32,4,32,1024]{3,2,1,0:T(8,128)(2,1)}), bf16[32,4,32,1024]{3,2,1,0:T(8,128)(2,1)}, u32[]{:S(2)}, u32[]{:S(2)}) async-start(bf16[32,4,32,1024]{3,2,1,0:T(8,128)(2,1)} %bitcast.194), calls=%async_computation.1 | async-start | bytes 16777216 | tf_op jit(solution)/shard_map/all_to_all | solution.py:72
  308.7 184.7 %all-to-all-done.1 = bf16[32,4,32,1024]{3,2,1,0:T(8,128)(2,1)} async-done(((bf16[32,4,32,1024]{3,2,1,0:T(8,128)(2,1)}), bf16[32,4,32,1024]{3,2,1,0:T(8,128)(2,1)}, u32[]{:S(2)}, u32[]{:S(2)}) %all-to-all-start.1) | async-done | bytes 8388640 | tf_op jit(solution)/shard_map/all_to_all | solution.py:72
  493.4 11.4 %copy.76 = bf16[1,4,32,32,1024]{4,3,2,1,0:T(8,128)(2,1)} copy(bf16[1,4,32,32,1024]{4,2,1,3,0:T(8,128)(2,1)} %bitcast.36) | data formatting | bytes 16777216 | tf_op jit(solution)/shard_map/all_to_all | solution.py:72
  504.8 13.4 %reshape.128 = bf16[4,32,32768]{2,1,0:T(8,128)(2,1)} reshape(bf16[1,4,32,32,1024]{4,3,2,1,0:T(8,128)(2,1)} %copy.76) | data formatting | bytes 16777216 | tf_op jit(solution)/shard_map/reshape | solution.py:79
  (54 shorter events, 23.8 us)
Async XLA Ops:
  5.9 53.0 %all-to-all-start.2 = ((s32[32,1,128]{2,1,0:T(1,128)}), s32[32,1,128]{2,1,0:T(1,128)S(1)}, u32[]{:S(2)}, u32[]{:S(2)}) async-start(s32[32,1,128]{2,1,0:T(1,128)} %reshape.167), calls=%async_computation.2 | async-start | bytes 32768 | tf_op jit(solution)/shard_map/all_to_all | solution.py:83
  58.8 5.9 %copy-start = (s32[32]{0:T(128)S(1)}, s32[32]{0:T(128)}, u32[]{:S(2)}) copy-start(s32[32]{0:T(128)} %param.8) | copy-start | bytes 388
  58.8 192.0 %all-to-all-start = ((bf16[32,128,1,1024]{1,3,2,0:T(8,128)(2,1)}), bf16[32,128,1,1024]{1,3,2,0:T(8,128)(2,1)}, u32[]{:S(2)}, u32[]{:S(2)}) async-start(bf16[32,128,1,1024]{1,3,2,0:T(8,128)(2,1)} %fusion), calls=%async_computation | async-start | bytes 16777216 | tf_op jit(solution)/shard_map/all_to_all | solution.py:51
  250.9 50.5 %all-to-all-start.3 = ((f32[1,128,256]{1,0,2:T(1,128)}), f32[1,128,256]{1,0,2:T(1,128)S(1)}, u32[]{:S(2)}, u32[]{:S(2)}) async-start(f32[1,128,256]{1,0,2:T(1,128)} %bitcast.49), calls=%async_computation.3 | async-start | bytes 262144 | tf_op jit(solution)/shard_map/all_to_all | solution.py:87
  301.4 192.0 %all-to-all-start.1 = ((bf16[32,4,32,1024]{3,2,1,0:T(8,128)(2,1)}), bf16[32,4,32,1024]{3,2,1,0:T(8,128)(2,1)}, u32[]{:S(2)}, u32[]{:S(2)}) async-start(bf16[32,4,32,1024]{3,2,1,0:T(8,128)(2,1)} %bitcast.194), calls=%async_computation.1 | async-start | bytes 16777216 | tf_op jit(solution)/shard_map/all_to_all | solution.py:72
